TPU v7x, 256 devices: a whole 4x4x8 slice. The times are simulated.
256 devices in a mesh: body: 16 (over z_hi, y), tile: 16 (over z_lo, x, core).
Axes of the slice: x: 4, y: 4, z: 8 (z_hi: 4, z_lo: 2; z = z_hi * 2 + z_lo), core: 2. Of those that a mesh axis runs over, the one named last changes fastest.
Arguments:
- panel_points: float32 [3, 131072], P(None, ('body', 'tile')), as said below
- normals: float32 [3, 131072], P(None, ('body', 'tile')), as said below
- weights: float32 [131072], P(('body', 'tile')), may hold values from 0.00024414062 to 0.0024414062
- counts: int32 [16], replicated, may hold values from 1024 to 8192, as said below
- source_points: float32 [3, 8192], replicated, as said below
- density: float32 [32, 131072], P(None, ('body', 'tile')), may hold values from -6 to 6
- incident: float32 [32, 131072], P(None, ('body', 'tile')), may hold values from -6 to 6
Outputs:
- density_next: float32 [32, 131072], P(None, ('body', 'tile'))
- amplitudes: float32 [32, 8192], P(None, 'body')
Inputs may be any that keep to these rules, and one draw needn't show every extreme that they name: `counts`: one body, drawn from the seed, has exactly 8192 live panels; every other body has between 1024 and 2730. `panel_points`: panels of body b lie within distance 1.2 of a centre on a lattice of spacing 3; normals are unit vectors. `normals`: unit vectors. `source_points`: sources of body b lie within distance 0.6 of the same centre.
All inputs are finite; a program needn't handle non-finite values.
Results may differ from a plain program's by a relative error of at most 0.0044.
Values may be sent and summed in bfloat16 or wider, within the bound.
A program may use at most 64 MiB of HBM per device.

v0:
```python
import math

import jax
import jax.numpy as jnp
from jax import lax
from jax.sharding import PartitionSpec as P

CORE_SQUARE = 0.01
WAVE = 3.0
COUPLING = 1.0


def copy_for_each(x, axis):
    peers = lax.axis_size(axis)
    return lax.all_to_all(jnp.broadcast_to(x[None], (peers, *x.shape)), axis, 0, 0, tiled=True)


def laid_out(parts, dim):
    lengths = list(parts.shape[1:])
    lengths[dim] *= parts.shape[0]
    return jnp.moveaxis(parts, 0, dim).reshape(lengths)


def collect(x, axis, dim):
    parts = copy_for_each(x, axis)
    return laid_out(parts, dim)


def over_copies(x, axis):
    everything = copy_for_each(x, axis)
    return jnp.sum(everything, axis=0)


def layer_tile(targets, sources):
    offset_vec = targets[:, None, :] - sources[:3, :, None]
    radius = jnp.sqrt(jnp.sum(offset_vec * offset_vec, 0) + CORE_SQUARE)
    inverse = 1.0 / radius
    slope = jnp.sum(offset_vec * sources[3:6, :, None], 0) * inverse
    phase = WAVE * radius
    cosine = jnp.cos(phase)
    sine = jnp.sin(phase)
    scaled = sources[6][:, None] * inverse
    real = scaled * (slope * (cosine * inverse + WAVE * sine) + COUPLING * sine)
    imaginary = scaled * (slope * (sine * inverse - WAVE * cosine) - COUPLING * cosine)
    return jnp.concatenate([real, imaginary], 1).astype(jnp.bfloat16)


def point_tile(targets, sources):
    offset_vec = targets[:, None, :] - sources[:3, :, None]
    radius = jnp.sqrt(jnp.sum(offset_vec * offset_vec, 0) + CORE_SQUARE)
    scaled = sources[3][:, None] / radius
    phase = WAVE * radius
    return jnp.concatenate([scaled * jnp.cos(phase), scaled * jnp.sin(phase)], 1).astype(
        jnp.bfloat16
    )


def kernel_product(maker, dens, sources, targets, total):
    count = dens.shape[1]
    size = math.gcd(count, 1024)
    turns = count // size

    def step(turn, running):
        source_block = lax.dynamic_slice_in_dim(sources, turn * size, size, 1)
        field_block = lax.dynamic_slice_in_dim(dens, turn * size, size, 1)
        return running + jnp.dot(
            field_block, maker(targets, source_block), preferred_element_type=jnp.float32
        )

    return lax.fori_loop(0, turns, step, total)


def complex_join(product, width):
    half = product.shape[-2] // 2
    upper = product[..., :half, :]
    lower = product[..., half:, :]
    real = upper[..., :width] - lower[..., width:]
    imaginary = upper[..., width:] + lower[..., :width]
    return jnp.concatenate([real, imaginary], -2)


def per_device(panel_points, normals, weights, counts, source_points, density, incident):
    channels, rows = density.shape
    group = lax.axis_index("body")
    place = lax.axis_index("tile")
    groups = lax.axis_size("body")
    cap = rows * lax.axis_size("tile")
    per_body = source_points.shape[1] // groups
    slots = place * rows + jnp.arange(rows, dtype=jnp.int32)
    limit = lax.dynamic_index_in_dim(counts, group, 0, keepdims=False)
    live = (slots < limit).astype(jnp.float32)
    weighted = weights * live
    geometry = jnp.concatenate(
        [panel_points, normals, weighted[None], jnp.zeros((1, rows), jnp.float32)], 0
    )
    geometry_all = collect(geometry, "tile", 1)
    sigma_start = density * live
    own_sources = lax.dynamic_slice_in_dim(source_points, group * per_body, per_body, 1)
    point_sources = jnp.concatenate([panel_points, weighted[None]], 0)
    raw_amplitude = kernel_product(
        point_tile,
        sigma_start.astype(jnp.bfloat16),
        point_sources,
        own_sources,
        jnp.zeros((channels, 2 * per_body), jnp.float32),
    )
    partial_amplitude = complex_join(raw_amplitude, per_body)
    amplitudes = over_copies(partial_amplitude, "tile")
    every_amplitude = collect(amplitudes.astype(jnp.bfloat16), "body", 1).astype(amplitudes.dtype)
    source_owner = jnp.arange(source_points.shape[1], dtype=jnp.int32) // per_body
    far = jnp.where(source_owner[None, :] == group, 0.0, every_amplitude).astype(jnp.bfloat16)
    source_geometry = jnp.concatenate(
        [source_points, jnp.ones((1, source_points.shape[1]), jnp.float32)], 0
    )
    raw_field = kernel_product(
        point_tile, far, source_geometry, panel_points, jnp.zeros((channels, 2 * rows), jnp.float32)
    )
    rhs = live * (incident - complex_join(raw_field, rows))
    size = math.gcd(cap, 1024)
    turns = cap // size
    turn_index = jnp.arange(turns, dtype=jnp.int32)

    def row_block(turn):
        return layer_tile(
            panel_points, lax.dynamic_slice_in_dim(geometry_all, turn * size, size, 1)
        )

    stored_rows = lax.map(row_block, turn_index).reshape(cap, 2 * rows)
    sigma = sigma_start
    for sweep_step in range(2):
        raw = jnp.dot(
            collect(sigma.astype(jnp.bfloat16), "tile", 1),
            stored_rows,
            preferred_element_type=jnp.float32,
        )
        sigma = live * (sigma + rhs - 0.5 * sigma - complex_join(raw, rows))
    return (sigma, amplitudes)


def solution(mesh):
    in_specs = (
        P(None, ("body", "tile")),
        P(None, ("body", "tile")),
        P(("body", "tile")),
        P(),
        P(),
        P(None, ("body", "tile")),
        P(None, ("body", "tile")),
    )
    out_specs = (P(None, ("body", "tile")), P(None, "body"))
    return jax.shard_map(
        per_device, mesh=mesh, in_specs=in_specs, out_specs=out_specs, check_vma=False
    )
```

profile of v0, /device:TPU:8, one launch (start us, length us, event | category | flops | bytes accessed | tf_op | source)
XLA Modules:
  0.0 346.1 jit_solution(3108726029396623382)
XLA Ops:
  0.6 1.3 dynamic_slice.32
  2.0 1.3 fusion.29
  4.8 5.8 %all-to-all-start.3 = ((f32[16,8,512]{2,1,0:T(8,128)}), f32[16,8,512]{2,1,0:T(8,128)S(1)}, u32[]{:S(2)}, u32[]{:S(2)}) async-start(f32[16,8,512]{2,1,0:T(8,128)} %broadcast_in_dim.51), calls=%async_computation.3 | async-start | bytes 524288 | tf_op jit(solution)/shard_map/all_to_all | solution.py:15
  12.0 1.1 multiply_reduce_fusion.1
  13.1 4.6 %multiply_convert_fusion.5 = (bf16[512,512]{1,0:T(8,128)(2,1)S(1)}, bf16[512,512]{1,0:T(8,128)(2,1)S(1)}) fusion(f32[512,512]{1,0:T(8,128)S(1)} %multiply_reduce_fusion.1, f32[512]{0:T(512)S(1)} %fusion.29), kind=kLoop, calls=%fused_computation.37 | loop fusion | flops 1835008 | bytes 2099200 | tf_op jit(solution)/shard_map/convert.8
  18.7 21.6 %all_to_all.25 = f32[16,32,512]{2,1,0:T(8,128)S(1)} all-to-all(f32[16,32,512]{2,1,0:T(8,128)S(1)} %broadcast_in_dim.45), channel_id=1, replica_groups=mesh['body'=16,'tile'=16] {'tile'}, dimensions={0} | all-to-all | bytes 2097152 | tf_op jit(solution)/shard_map/all_to_all | solution.py:15
  40.3 0.9 broadcast_in_dim.47
  41.2 3.7 %all-to-all-start.2 = ((bf16[16,32,512]{2,1,0:T(8,128)(2,1)}), bf16[16,32,512]{2,1,0:T(8,128)(2,1)S(1)}, u32[]{:S(2)}, u32[]{:S(2)}) async-start(bf16[16,32,512]{2,1,0:T(8,128)(2,1)} %broadcast_in_dim.47), calls=%async_computation.2 | async-start | bytes 1048576 | tf_op jit(solution)/shard_map/all_to_all | solution.py:15
  46.3 9.4 %all-to-all-done.2 = bf16[16,32,512]{2,1,0:T(8,128)(2,1)S(1)} async-done(((bf16[16,32,512]{2,1,0:T(8,128)(2,1)}), bf16[16,32,512]{2,1,0:T(8,128)(2,1)S(1)}, u32[]{:S(2)}, u32[]{:S(2)}) %all-to-all-start.2) | async-done | bytes 524320 | tf_op jit(solution)/shard_map/all_to_all | solution.py:15
  56.6 10.7 %all-to-all-start.1 = ((bf16[16,32,512]{2,1,0:T(8,128)(2,1)}), bf16[16,32,512]{2,1,0:T(8,128)(2,1)S(1)}, u32[]{:S(2)}, u32[]{:S(2)}) async-start(bf16[16,32,512]{2,1,0:T(8,128)(2,1)} %broadcast_in_dim.46), calls=%async_computation.1 | async-start | bytes 1048576 | tf_op jit(solution)/shard_map/all_to_all | solution.py:15
  67.2 133.8 %while.29 = (s32[]{:T(128)}, bf16[8,1024,1024]{2,1,0:T(8,128)(2,1)}, s32[8]{0:T(128)S(1)}, f32[8,8192]{1,0:T(8,128)S(1)}, f32[3,512]{1,0:T(4,128)S(1)}, /*index=...) while((s32[]{:T(128)}, bf16[8,1024,1024]{2,1,0:T(8,128)(2,1)}, s32[8]{0:T(128)S(1)}, ...), condition=%wide.region_8.9_spmd, body=%wide.region_5.8_spmd.sunk | while | flops 20971528 | bytes 14772439 | solution.py:128
  68.5 2.9 fusion.48
  71.4 10.9 %fusion.49 = (bf16[1,1024,512]{2,1,0:T(8,128)(2,1)S(1)}, bf16[1,1024,512]{2,1,0:T(8,128)(2,1)S(1)}) fusion(f32[1024,512]{1,0:T(8,128)} %get-tuple-element.268, f32[1024,512]{1,0:T(8,128)S(1)} %get-tuple-element.269, f32[1024]{0:T(1024)S(1)} %bitcast.48), kind=kLoop, calls=%fused_computation.12.clone.1 | loop fusion | flops 9961472 | bytes 6295552 | tf_op jit(solution)/shard_map/while/body/eval_jaxpr/concatenate | solution.py:45
  82.4 1.6 maximum_dynamic-update-slice_fusion.2
  85.2 2.9 fusion.48
  88.2 10.9 %fusion.49 = (bf16[1,1024,512]{2,1,0:T(8,128)(2,1)S(1)}, bf16[1,1024,512]{2,1,0:T(8,128)(2,1)S(1)}) fusion(f32[1024,512]{1,0:T(8,128)} %get-tuple-element.268, f32[1024,512]{1,0:T(8,128)S(1)} %get-tuple-element.269, f32[1024]{0:T(1024)S(1)} %bitcast.48), kind=kLoop, calls=%fused_computation.12.clone.1 | loop fusion | flops 9961472 | bytes 6295552 | tf_op jit(solution)/shard_map/while/body/eval_jaxpr/concatenate | solution.py:45
  99.1 1.6 maximum_dynamic-update-slice_fusion.2
  101.9 2.9 fusion.48
  104.9 10.9 %fusion.49 = (bf16[1,1024,512]{2,1,0:T(8,128)(2,1)S(1)}, bf16[1,1024,512]{2,1,0:T(8,128)(2,1)S(1)}) fusion(f32[1024,512]{1,0:T(8,128)} %get-tuple-element.268, f32[1024,512]{1,0:T(8,128)S(1)} %get-tuple-element.269, f32[1024]{0:T(1024)S(1)} %bitcast.48), kind=kLoop, calls=%fused_computation.12.clone.1 | loop fusion | flops 9961472 | bytes 6295552 | tf_op jit(solution)/shard_map/while/body/eval_jaxpr/concatenate | solution.py:45
  115.8 1.6 maximum_dynamic-update-slice_fusion.2
  118.6 2.9 fusion.48
  121.6 10.9 %fusion.49 = (bf16[1,1024,512]{2,1,0:T(8,128)(2,1)S(1)}, bf16[1,1024,512]{2,1,0:T(8,128)(2,1)S(1)}) fusion(f32[1024,512]{1,0:T(8,128)} %get-tuple-element.268, f32[1024,512]{1,0:T(8,128)S(1)} %get-tuple-element.269, f32[1024]{0:T(1024)S(1)} %bitcast.48), kind=kLoop, calls=%fused_computation.12.clone.1 | loop fusion | flops 9961472 | bytes 6295552 | tf_op jit(solution)/shard_map/while/body/eval_jaxpr/concatenate | solution.py:45
  132.5 1.6 maximum_dynamic-update-slice_fusion.2
  135.4 2.9 fusion.48
  138.3 10.9 %fusion.49 = (bf16[1,1024,512]{2,1,0:T(8,128)(2,1)S(1)}, bf16[1,1024,512]{2,1,0:T(8,128)(2,1)S(1)}) fusion(f32[1024,512]{1,0:T(8,128)} %get-tuple-element.268, f32[1024,512]{1,0:T(8,128)S(1)} %get-tuple-element.269, f32[1024]{0:T(1024)S(1)} %bitcast.48), kind=kLoop, calls=%fused_computation.12.clone.1 | loop fusion | flops 9961472 | bytes 6295552 | tf_op jit(solution)/shard_map/while/body/eval_jaxpr/concatenate | solution.py:45
  149.3 1.6 maximum_dynamic-update-slice_fusion.2
  152.1 2.9 fusion.48
  155.1 10.9 %fusion.49 = (bf16[1,1024,512]{2,1,0:T(8,128)(2,1)S(1)}, bf16[1,1024,512]{2,1,0:T(8,128)(2,1)S(1)}) fusion(f32[1024,512]{1,0:T(8,128)} %get-tuple-element.268, f32[1024,512]{1,0:T(8,128)S(1)} %get-tuple-element.269, f32[1024]{0:T(1024)S(1)} %bitcast.48), kind=kLoop, calls=%fused_computation.12.clone.1 | loop fusion | flops 9961472 | bytes 6295552 | tf_op jit(solution)/shard_map/while/body/eval_jaxpr/concatenate | solution.py:45
  166.1 1.6 maximum_dynamic-update-slice_fusion.2
  168.8 2.9 fusion.48
  171.8 10.9 %fusion.49 = (bf16[1,1024,512]{2,1,0:T(8,128)(2,1)S(1)}, bf16[1,1024,512]{2,1,0:T(8,128)(2,1)S(1)}) fusion(f32[1024,512]{1,0:T(8,128)} %get-tuple-element.268, f32[1024,512]{1,0:T(8,128)S(1)} %get-tuple-element.269, f32[1024]{0:T(1024)S(1)} %bitcast.48), kind=kLoop, calls=%fused_computation.12.clone.1 | loop fusion | flops 9961472 | bytes 6295552 | tf_op jit(solution)/shard_map/while/body/eval_jaxpr/concatenate | solution.py:45
  182.8 1.6 maximum_dynamic-update-slice_fusion.2
  185.6 2.9 fusion.48
  188.5 10.9 %fusion.49 = (bf16[1,1024,512]{2,1,0:T(8,128)(2,1)S(1)}, bf16[1,1024,512]{2,1,0:T(8,128)(2,1)S(1)}) fusion(f32[1024,512]{1,0:T(8,128)} %get-tuple-element.268, f32[1024,512]{1,0:T(8,128)S(1)} %get-tuple-element.269, f32[1024]{0:T(1024)S(1)} %bitcast.48), kind=kLoop, calls=%fused_computation.12.clone.1 | loop fusion | flops 9961472 | bytes 6295552 | tf_op jit(solution)/shard_map/while/body/eval_jaxpr/concatenate | solution.py:45
  199.5 1.6 maximum_dynamic-update-slice_fusion.2
  201.1 8.8 %fusion.34 = f32[32,1024]{1,0:T(8,128)S(1)} fusion(bf16[32,8192]{1,0:T(8,128)(2,1)S(1)} %bitcast.40, bf16[8192,1024]{1,0:T(8,128)(2,1)} %bitcast.38), kind=kOutput, calls=%fused_computation.72 | convolution fusion | flops 536870912 | bytes 17432576 | tf_op jit(solution)/shard_map/dot_general | solution.py:131
  210.0 0.9 select_convert_fusion
  210.9 112.1 %while.30 = (s32[]{:T(128)}, f32[32,1024]{1,0:T(8,128)S(1)}, bf16[32,8192]{1,0:T(8,128)(2,1)}, f32[4,8192]{1,0:T(4,128)}, f32[3,512]{1,0:T(4,128)S(1)}, /*index=...) while((s32[]{:T(128)}, f32[32,1024]{1,0:T(8,128)S(1)}, bf16[32,8192]{1,0:T(8,128)(2,1)}, ...), condition=%wide.region_4.5_spmd.clone, body=%wide.region_2.0_spmd.clone.sunk | while | flops 79233032 | bytes 8771773 | solution.py:70
  211.6 0.9 multiply_reduce_fusion.3
  213.4 9.8 %multiply_convert_fusion.8 = (bf16[1024,512]{1,0:T(8,128)(2,1)S(1)}, bf16[1024,512]{1,0:T(8,128)(2,1)}) fusion(f32[1024,512]{1,0:T(8,128)S(1)} %multiply_reduce_fusion.3, f32[1024]{0:T(1024)S(1)} %bitcast.47), kind=kLoop, calls=%fused_computation.21.clone.1 | loop fusion | flops 3670016 | bytes 4198400 | tf_op jit(solution)/shard_map/convert.4
  223.2 1.7 fusion.52
  225.7 0.9 multiply_reduce_fusion.3
  227.4 9.8 %multiply_convert_fusion.8 = (bf16[1024,512]{1,0:T(8,128)(2,1)S(1)}, bf16[1024,512]{1,0:T(8,128)(2,1)}) fusion(f32[1024,512]{1,0:T(8,128)S(1)} %multiply_reduce_fusion.3, f32[1024]{0:T(1024)S(1)} %bitcast.47), kind=kLoop, calls=%fused_computation.21.clone.1 | loop fusion | flops 3670016 | bytes 4198400 | tf_op jit(solution)/shard_map/convert.4
  237.2 1.7 fusion.52
  239.7 0.9 multiply_reduce_fusion.3
  241.4 9.8 %multiply_convert_fusion.8 = (bf16[1024,512]{1,0:T(8,128)(2,1)S(1)}, bf16[1024,512]{1,0:T(8,128)(2,1)}) fusion(f32[1024,512]{1,0:T(8,128)S(1)} %multiply_reduce_fusion.3, f32[1024]{0:T(1024)S(1)} %bitcast.47), kind=kLoop, calls=%fused_computation.21.clone.1 | loop fusion | flops 3670016 | bytes 4198400 | tf_op jit(solution)/shard_map/convert.4
  251.2 1.7 fusion.52
  253.7 0.9 multiply_reduce_fusion.3
  255.4 9.8 %multiply_convert_fusion.8 = (bf16[1024,512]{1,0:T(8,128)(2,1)S(1)}, bf16[1024,512]{1,0:T(8,128)(2,1)}) fusion(f32[1024,512]{1,0:T(8,128)S(1)} %multiply_reduce_fusion.3, f32[1024]{0:T(1024)S(1)} %bitcast.47), kind=kLoop, calls=%fused_computation.21.clone.1 | loop fusion | flops 3670016 | bytes 4198400 | tf_op jit(solution)/shard_map/convert.4
  265.2 1.7 fusion.52
  267.7 0.9 multiply_reduce_fusion.3
  269.4 9.8 %multiply_convert_fusion.8 = (bf16[1024,512]{1,0:T(8,128)(2,1)S(1)}, bf16[1024,512]{1,0:T(8,128)(2,1)}) fusion(f32[1024,512]{1,0:T(8,128)S(1)} %multiply_reduce_fusion.3, f32[1024]{0:T(1024)S(1)} %bitcast.47), kind=kLoop, calls=%fused_computation.21.clone.1 | loop fusion | flops 3670016 | bytes 4198400 | tf_op jit(solution)/shard_map/convert.4
  279.2 1.7 fusion.52
  281.7 0.9 multiply_reduce_fusion.3
  283.5 9.8 %multiply_convert_fusion.8 = (bf16[1024,512]{1,0:T(8,128)(2,1)S(1)}, bf16[1024,512]{1,0:T(8,128)(2,1)}) fusion(f32[1024,512]{1,0:T(8,128)S(1)} %multiply_reduce_fusion.3, f32[1024]{0:T(1024)S(1)} %bitcast.47), kind=kLoop, calls=%fused_computation.21.clone.1 | loop fusion | flops 3670016 | bytes 4198400 | tf_op jit(solution)/shard_map/convert.4
  293.2 1.7 fusion.52
  295.7 0.9 multiply_reduce_fusion.3
  297.5 9.8 %multiply_convert_fusion.8 = (bf16[1024,512]{1,0:T(8,128)(2,1)S(1)}, bf16[1024,512]{1,0:T(8,128)(2,1)}) fusion(f32[1024,512]{1,0:T(8,128)S(1)} %multiply_reduce_fusion.3, f32[1024]{0:T(1024)S(1)} %bitcast.47), kind=kLoop, calls=%fused_computation.21.clone.1 | loop fusion | flops 3670016 | bytes 4198400 | tf_op jit(solution)/shard_map/convert.4
  307.2 1.7 fusion.52
  309.7 0.9 multiply_reduce_fusion.3
  311.5 9.8 %multiply_convert_fusion.8 = (bf16[1024,512]{1,0:T(8,128)(2,1)S(1)}, bf16[1024,512]{1,0:T(8,128)(2,1)}) fusion(f32[1024,512]{1,0:T(8,128)S(1)} %multiply_reduce_fusion.3, f32[1024]{0:T(1024)S(1)} %bitcast.47), kind=kLoop, calls=%fused_computation.21.clone.1 | loop fusion | flops 3670016 | bytes 4198400 | tf_op jit(solution)/shard_map/convert.4
  321.3 1.7 fusion.52
  323.1 13.5 %all_to_all.26 = bf16[16,32,512]{2,1,0:T(8,128)(2,1)S(1)} all-to-all(bf16[16,32,512]{2,1,0:T(8,128)(2,1)S(1)} %broadcast_in_dim.52), channel_id=1, replica_groups=mesh['body'=16,'tile'=16] {'tile'}, dimensions={0} | all-to-all | bytes 1048576 | tf_op jit(solution)/shard_map/all_to_all | solution.py:15
  336.6 8.8 %fusion.35 = f32[32,1024]{1,0:T(8,128)S(1)} fusion(bf16[32,8192]{1,0:T(8,128)(2,1)S(1)} %bitcast.41, bf16[8192,1024]{1,0:T(8,128)(2,1)} %bitcast.39), kind=kOutput, calls=%fused_computation.73 | convolution fusion | flops 536870912 | bytes 17432576 | tf_op jit(solution)/shard_map/dot_general | solution.py:131
  (82 shorter events, 25.0 us)
Async XLA Ops:
  0.6 17.1 %copy-start.1 = (f32[32,512]{1,0:T(8,128)S(1)}, f32[32,512]{1,0:T(8,128)}, u32[]{:S(2)}) copy-start(f32[32,512]{1,0:T(8,128)} %param.16) | copy-start | bytes 196612
  4.8 13.8 %all-to-all-start.3 = ((f32[16,8,512]{2,1,0:T(8,128)}), f32[16,8,512]{2,1,0:T(8,128)S(1)}, u32[]{:S(2)}, u32[]{:S(2)}) async-start(f32[16,8,512]{2,1,0:T(8,128)} %broadcast_in_dim.51), calls=%async_computation.3 | async-start | bytes 524288 | tf_op jit(solution)/shard_map/all_to_all | solution.py:15
  18.7 26.2 %copy-start.4 = (f32[3,8192]{1,0:T(4,128)S(1)}, f32[3,8192]{1,0:T(4,128)}, u32[]{:S(2)}) copy-start(f32[3,8192]{1,0:T(4,128)} %param.15) | copy-start | bytes 294916
  41.2 26.0 %copy-start = (f32[3,512]{1,0:T(4,128)S(1)}, f32[3,512]{1,0:T(4,128)}, u32[]{:S(2)}) copy-start(f32[3,512]{1,0:T(4,128)} %param.11) | copy-start | bytes 18436
  41.2 14.5 %all-to-all-start.2 = ((bf16[16,32,512]{2,1,0:T(8,128)(2,1)}), bf16[16,32,512]{2,1,0:T(8,128)(2,1)S(1)}, u32[]{:S(2)}, u32[]{:S(2)}) async-start(bf16[16,32,512]{2,1,0:T(8,128)(2,1)} %broadcast_in_dim.47), calls=%async_computation.2 | async-start | bytes 1048576 | tf_op jit(solution)/shard_map/all_to_all | solution.py:15
  46.3 20.9 %copy-start.2 = (f32[32,512]{1,0:T(8,128)}, f32[32,512]{1,0:T(8,128)S(1)}, u32[]{:S(2)}) copy-start(f32[32,512]{1,0:T(8,128)S(1)} %reduce_sum.51) | copy-start | bytes 196612
  56.6 153.3 %all-to-all-start.1 = ((bf16[16,32,512]{2,1,0:T(8,128)(2,1)}), bf16[16,32,512]{2,1,0:T(8,128)(2,1)S(1)}, u32[]{:S(2)}, u32[]{:S(2)}) async-start(bf16[16,32,512]{2,1,0:T(8,128)(2,1)} %broadcast_in_dim.46), calls=%async_computation.1 | async-start | bytes 1048576 | tf_op jit(solution)/shard_map/all_to_all | solution.py:15
  201.1 8.9 %copy-start.6 = (pred[8192]{0:T(1024)(128)(4,1)S(1)}, pred[8192]{0:T(1024)(128)(4,1)}, u32[]{:S(2)}) copy-start(pred[8192]{0:T(1024)(128)(4,1)} %fusion.25) | copy-start | bytes 24580
  209.9 1.0 copy-start.5
  210.9 112.2 %copy-start.3 = (f32[32,512]{1,0:T(8,128)S(1)}, f32[32,512]{1,0:T(8,128)}, u32[]{:S(2)}) copy-start(f32[32,512]{1,0:T(8,128)} %param.17) | copy-start | bytes 196612
where the time goes:
time: 348 us; the launch traced here: 346 us
  other arithmetic  220 us (63%)
  blocking collectives  35 us (10%)
  matrix products  31.7 us (9%)
  local copies, waits for them, and re-layouts  23.4 us (7%)
  starting transfers between devices  20.1 us (6%)
  waiting for transfers between devices  9.9 us (3%)
  loops' own time  4.83 us (1%)
    concatenate x8, other arithmetic, layer_tile(): return jnp.concatenate([real, imaginary], 1).astype(jnp.bfloat16)  87.6 us
    another operation x9, other arithmetic  82.8 us
    all_to_all x2, blocking collectives, copy_for_each(): lax.all_to_all(jnp.broadcast_to(x[None], (peers, *x.shape)), axis, 0, 0,...  35 us
    reduce_sum x8, other arithmetic, layer_tile(): radius = jnp.sqrt(jnp.sum(offset_vec * offset_vec, 0) + CORE_SQUARE)  23.2 us
    all_to_all x3, starting transfers between devices, copy_for_each(): lax.all_to_all(jnp.broadcast_to(x[None], (peers, *x.shape)), axis, 0, 0,...  20.1 us
    dot_general x2, matrix products, per_device(): jnp.dot(collect(sigma.astype(jnp.bfloat16), 'tile', 1), stored_rows, pref...  17.5 us
    dot_general x9, matrix products, step(): jnp.dot(field_block, maker(targets, source_block), preferred_element_type...  14.2 us
    dynamic_update_slice x8, other arithmetic, per_device(): stored_rows = lax.map(row_block, turn_index).reshape(cap, 2 * rows)  12.8 us
  transfers between devices with their start and end apart: 3, of which 2 were waited for; matrix products, arithmetic and copies ran while one was open for 42% of the time, Pallas kernels for 0%

commit v1 on v0

v1 whole, which is shorter than its diff:
```python
import functools
import math

import jax
import jax.numpy as jnp
from jax import lax
from jax.experimental import pallas as pl
from jax.experimental.pallas import tpu as pltpu
from jax.sharding import PartitionSpec as P

KAPPA = 3.0/(2*math.pi)
S3=(4.442867903030504, -7.307443421264801, 3.5947880783718604, -0.7843740306771035)
BF=jnp.bfloat16; F32=jnp.float32

def pieces(v):
    h=v.astype(BF).astype(F32); r=v-h
    m=r.astype(BF).astype(F32)
    return h,m,r-m
def pick(rows,a,b,c,d,e,f):
    z=jnp.zeros_like(rows,dtype=F32)
    for k,v in enumerate((a,b,c,d,e,f)):
        z=jnp.where(rows==k,v,z)
    return z
def dot3(a,b):
    return jnp.broadcast_to(jnp.sum(a*b,axis=0,keepdims=True),a.shape)
def target_features(x):
    h,m,l=pieces(x); a,b,c=pieces(dot3(x,x))
    rows=lax.broadcasted_iota(jnp.int32,x.shape,0)
    tail=pick(rows,a,b,c,1.0,1.0,1.0)
    return jnp.concatenate([h,h,h,m,m,l,tail,jnp.zeros_like(tail)],0).astype(BF)
def source_features(y):
    h,m,l=pieces(-2.0*y); a,b,c=pieces(dot3(y,y)+0.01*KAPPA*KAPPA)
    rows=lax.broadcasted_iota(jnp.int32,y.shape,0)
    tail=pick(rows,1.0,1.0,1.0,a,b,c)
    return jnp.concatenate([h,m,l,h,m,h,tail,jnp.zeros_like(tail)],0).astype(BF)
def normal_features(n,y):
    h,m,l=pieces(n); a,b,c=pieces(-dot3(n,y))
    rows=lax.broadcasted_iota(jnp.int32,y.shape,0)
    tail=pick(rows,0.0,0.0,0.0,a,b,c)
    return jnp.concatenate([h,m,l,h,m,h,tail,jnp.zeros_like(tail)],0).astype(BF)
def cross(a,b):
    return lax.dot_general(a,b,(((0,),(0,)),((),())),preferred_element_type=F32)
def wave(u):
    inv=lax.rsqrt(u); turn=u*inv
    f=turn-jnp.round(turn); z=f*f
    s=f*(((S3[3]*z+S3[2])*z+S3[1])*z+S3[0])
    q=s*s
    b=jnp.maximum(2.0-q,1e-30)
    return inv,1.0-q,s*(b*lax.rsqrt(b))
def point_values(u):
    inv,c,s=wave(u)
    return (c*inv).astype(BF),(s*inv).astype(BF)
def layer_values(u,p):
    inv,c,s=wave(u)
    e=p*(inv*inv); g=inv+e; h=e*(inv*(1/(2*math.pi)))
    return (c*h+s*g).astype(BF),(s*h-c*g).astype(BF)

def field_kernel(tgt,src,dens,out,feat,ubuf,kbuf,acc,*,blk):
    T=tgt.shape[1]; n=src.shape[1]//blk; half=256; nh=T//half
    feat[...]=target_features(tgt[...])
    acc[...]=jnp.zeros_like(acc)
    kbuf[...]=jnp.zeros_like(kbuf)
    def fill(i,slot):
        y=src[:,pl.ds(pl.multiple_of(i*blk,blk),blk)]
        A=source_features(y)
        for th in range(nh):
            ubuf[slot,:,th*half:(th+1)*half]=cross(A,feat[:,th*half:(th+1)*half])
    def evaluate(slot):
        for th in range(nh):
            for ch in range(blk//16):
                u=ubuf[slot,ch*16:(ch+1)*16,th*half:(th+1)*half]
                re,im=point_values(u)
                kbuf[slot,ch*16:(ch+1)*16,th*half:(th+1)*half]=re
                kbuf[slot,ch*16:(ch+1)*16,T+th*half:T+(th+1)*half]=im
    def contract(i,slot):
        d=dens[:,pl.ds(pl.multiple_of(i*blk,blk),blk)]
        acc[...]+=jnp.dot(d,kbuf[slot],preferred_element_type=F32)
    fill(0,0)
    def body(k,_):
        i=2*k
        for par in range(2):
            fill(jnp.minimum(i+par+1,n-1),1-par)
            evaluate(par)
            contract(jnp.maximum(i+par-1,0),1-par)
        return 0
    lax.fori_loop(0,n//2,body,0)
    contract(n-1,1)
    out[...]=acc[...]
def field(tgt,src,dens,blk=256):
    T=tgt.shape[1]
    return pl.pallas_call(functools.partial(field_kernel,blk=blk),out_shape=jax.ShapeDtypeStruct((32,2*T),F32),
      scratch_shapes=[pltpu.VMEM((64,T),BF),pltpu.VMEM((2,blk,T),F32),pltpu.VMEM((2,blk,2*T),BF),pltpu.VMEM((32,2*T),F32)],
      compiler_params=pltpu.CompilerParams(vmem_limit_bytes=60*2**20))(tgt,src,dens)

def layer_kernel(tgt,src,nrm,dens,out,kout,feat,ubuf,pbuf,acc,*,blk):
    T=tgt.shape[1]; n=src.shape[1]//blk; half=256; nh=T//half
    feat[...]=target_features(tgt[...])
    acc[...]=jnp.zeros_like(acc)
    def fill(i,slot):
        y=src[:,pl.ds(pl.multiple_of(i*blk,blk),blk)]
        nn=nrm[:,pl.ds(pl.multiple_of(i*blk,blk),blk)]
        A=source_features(y); N=normal_features(nn,y)
        for th in range(nh):
            ubuf[slot,:,th*half:(th+1)*half]=cross(A,feat[:,th*half:(th+1)*half])
            pbuf[slot,:,th*half:(th+1)*half]=cross(N,feat[:,th*half:(th+1)*half])
    def evaluate(i,slot):
        for th in range(nh):
            for ch in range(blk//16):
                sl=(slot,slice(ch*16,(ch+1)*16),slice(th*half,(th+1)*half))
                re,im=layer_values(ubuf[sl],pbuf[sl])
                r=pl.ds(pl.multiple_of(i*blk+ch*16,16),16)
                kout[r,th*half:(th+1)*half]=re
                kout[r,T+th*half:T+(th+1)*half]=im
    def contract(i):
        o=pl.multiple_of(i*blk,blk)
        acc[...]+=jnp.dot(dens[:,pl.ds(o,blk)],kout[pl.ds(o,blk),:],preferred_element_type=F32)
    fill(0,0)
    kout[(n-1)*blk:,:]=jnp.zeros((blk,2*T),BF)
    def body(k,_):
        i=2*k
        for par in range(2):
            fill(jnp.minimum(i+par+1,n-1),1-par)
            evaluate(i+par,par)
            j=i+par-1
            contract(jnp.where(j<0,n-1,j))
        return 0
    lax.fori_loop(0,n//2,body,0)
    contract(n-1)
    out[...]=acc[...]
def layer(tgt,src,nrm,dens,blk=256):
    T=tgt.shape[1]
    return pl.pallas_call(functools.partial(layer_kernel,blk=blk),out_shape=(jax.ShapeDtypeStruct((32,2*T),F32),jax.ShapeDtypeStruct((src.shape[1],2*T),BF)),
      scratch_shapes=[pltpu.VMEM((64,T),BF),pltpu.VMEM((2,blk,T),F32),pltpu.VMEM((2,blk,T),F32),pltpu.VMEM((32,2*T),F32)],
      compiler_params=pltpu.CompilerParams(vmem_limit_bytes=60*2**20))(tgt,src,nrm,dens)


def copy_for_each(x, axis):
    peers = lax.axis_size(axis)
    return lax.all_to_all(jnp.broadcast_to(x[None], (peers, *x.shape)), axis, 0, 0, tiled=True)


def laid_out(parts, dim):
    lengths = list(parts.shape[1:])
    lengths[dim] *= parts.shape[0]
    return jnp.moveaxis(parts, 0, dim).reshape(lengths)


def collect(x, axis, dim):
    parts = copy_for_each(x, axis)
    return laid_out(parts, dim)


def over_copies(x, axis):
    everything = copy_for_each(x, axis)
    return jnp.sum(everything, axis=0)


def complex_join(product, width):
    half = product.shape[-2] // 2
    upper = product[..., :half, :]
    lower = product[..., half:, :]
    real = upper[..., :width] - lower[..., width:]
    imaginary = upper[..., width:] + lower[..., :width]
    return jnp.concatenate([real, imaginary], -2)


def image_kernel(dens, kin, out, acc):
    i = pl.program_id(0)

    @pl.when(i == 0)
    def _():
        acc[...] = jnp.zeros_like(acc)

    acc[...] += jnp.dot(dens[...], kin[...], preferred_element_type=F32)

    @pl.when(i == pl.num_programs(0) - 1)
    def _():
        out[...] = acc[...]


def image(dens, kin):
    n, w = kin.shape
    return pl.pallas_call(
        image_kernel,
        grid=(n // 1024,),
        in_specs=[pl.BlockSpec((32, 1024), lambda i: (0, i)), pl.BlockSpec((1024, w), lambda i: (i, 0))],
        out_specs=pl.BlockSpec((32, w), lambda i: (0, 0)),
        out_shape=jax.ShapeDtypeStruct((32, w), F32),
        scratch_shapes=[pltpu.VMEM((32, w), F32)],
    )(dens, kin)


def eight(a):
    return jnp.concatenate([a, jnp.zeros((5, a.shape[1]), F32)], 0)


def per_device(panel_points, normals, weights, counts, source_points, density, incident):
    channels, rows = density.shape
    group = lax.axis_index("body")
    place = lax.axis_index("tile")
    groups = lax.axis_size("body")
    per_body = source_points.shape[1] // groups
    slots = place * rows + jnp.arange(rows, dtype=jnp.int32)
    limit = lax.dynamic_index_in_dim(counts, group, 0, keepdims=False)
    live = (slots < limit).astype(F32)
    scale = KAPPA * weights * live
    own = lax.dynamic_slice_in_dim(source_points, group * per_body, per_body, 1)
    centre = own[:, :1]
    mine = eight(KAPPA * (panel_points - centre))
    geometry = jnp.concatenate([mine, eight(3.0 * normals)], 0)
    geometry_all = collect(geometry, "tile", 1)
    sigma_start = density * live

    def loaded(sigma):
        return (scale * sigma.astype(BF).astype(F32)).astype(BF)

    first = loaded(sigma_start)
    raw_amplitude = field(eight(KAPPA * (own - centre)), mine, first)
    amplitudes = over_copies(complex_join(raw_amplitude, per_body), "tile")
    every = collect(amplitudes.astype(BF), "body", 1)
    source_owner = jnp.arange(source_points.shape[1], dtype=jnp.int32) // per_body
    far = jnp.where(source_owner[None, :] == group, jnp.zeros_like(every), every)
    raw, stored = layer(mine, geometry_all[:8], geometry_all[8:], collect(first, "tile", 1))
    raw_field = field(mine, eight(KAPPA * (source_points - centre)), far)
    rhs = live * (incident - KAPPA * complex_join(raw_field, rows))
    sigma = live * (sigma_start + rhs - 0.5 * sigma_start - complex_join(raw, rows))
    raw = image(collect(loaded(sigma), "tile", 1), stored)
    sigma = live * (sigma + rhs - 0.5 * sigma - complex_join(raw, rows))
    return (sigma, amplitudes)


def solution(mesh):
    in_specs = (
        P(None, ("body", "tile")),
        P(None, ("body", "tile")),
        P(("body", "tile")),
        P(),
        P(),
        P(None, ("body", "tile")),
        P(None, ("body", "tile")),
    )
    out_specs = (P(None, ("body", "tile")), P(None, "body"))
    return jax.shard_map(
        per_device, mesh=mesh, in_specs=in_specs, out_specs=out_specs, check_vma=False
    )
```

time: 348 us -> 155 us (0.45)
  other arithmetic: 220 us -> 9.58 us
  Pallas kernels: 0 us -> 64.2 us
  matrix products: 31.7 us -> 0 us
  waiting for transfers between devices: 9.9 us -> 31.7 us
  blocking collectives: 35 us -> 13.5 us
  local copies, waits for them, and re-layouts: 23.4 us -> 10.4 us
  loops' own time: 4.83 us -> 0 us
  starting transfers between devices: 20.1 us -> 23.6 us
    concatenate x9 -> x1, other arithmetic: 88.4 us -> 0.01 us  [per_device(): geometry = jnp.concatenate([mine, eight(3.0 * normals)], 0)]
    another operation x9 -> x0, other arithmetic: 82.8 us -> none
    pallas_call x0 -> x4, Pallas kernels: none -> 64.2 us  [the longest x1 32 us: layer(): pl.pallas_call(functools.partial(layer_kernel, blk=blk), out_shape=(jax.S...]
    reduce_sum x17 -> x0, other arithmetic: 31.8 us -> none  [the longest x8 23.2 us: layer_tile(): radius = jnp.sqrt(jnp.sum(offset_vec * offset_vec, 0) + CORE_SQUARE)]
    dot_general x11 -> x0, matrix products: 31.7 us -> none  [the longest x2 17.5 us: per_device(): jnp.dot(collect(sigma.astype(jnp.bfloat16), 'tile', 1), stored_rows, pref...]
    all_to_all x3 -> x4, waiting for transfers between devices: 9.9 us -> 31.7 us  [copy_for_each(): lax.all_to_all(jnp.broadcast_to(x[None], (peers, *x.shape)), axis, 0, 0,...]
    all_to_all x2 -> x1, blocking collectives: 35 us -> 13.5 us  [copy_for_each(): lax.all_to_all(jnp.broadcast_to(x[None], (peers, *x.shape)), axis, 0, 0,...]
    dynamic_update_slice x8 -> x0, other arithmetic: 12.8 us -> none  [per_device(): stored_rows = lax.map(row_block, turn_index).reshape(cap, 2 * rows)]
  transfers between devices with their start and end apart: 3 -> 4, of which waited for: 2 -> 3; matrix products, arithmetic and copies ran while one was open for 42% -> 5% of each run, Pallas kernels for 0% -> 22%
where the time goes in v1:
time: 155 us; the launch traced here: 154 us
  Pallas kernels  64.2 us (41%)
  waiting for transfers between devices  31.7 us (20%)
  starting transfers between devices  23.6 us (15%)
  blocking collectives  13.5 us (9%)
  local copies, waits for them, and re-layouts  10.4 us (7%)
  other arithmetic  9.58 us (6%)
    pallas_call x1, Pallas kernels, layer(): pl.pallas_call(functools.partial(layer_kernel, blk=blk), out_shape=(jax.S...  32 us
    all_to_all x4, waiting for transfers between devices, copy_for_each(): lax.all_to_all(jnp.broadcast_to(x[None], (peers, *x.shape)), axis, 0, 0,...  31.7 us
    all_to_all x4, starting transfers between devices, copy_for_each(): lax.all_to_all(jnp.broadcast_to(x[None], (peers, *x.shape)), axis, 0, 0,...  23.6 us
    pallas_call x2, Pallas kernels, field(): pl.pallas_call(functools.partial(field_kernel, blk=blk), out_shape=jax.Sh...  22.1 us
    all_to_all x1, blocking collectives, copy_for_each(): lax.all_to_all(jnp.broadcast_to(x[None], (peers, *x.shape)), axis, 0, 0,...  13.5 us
    pallas_call x1, Pallas kernels, image(): pl.pallas_call(image_kernel, grid=(n // 1024,), in_specs=[pl.BlockSpec((3...  10.1 us
    broadcast_in_dim x5, local copies, waits for them, and re-layouts, copy_for_each(): jnp.broadcast_to(x[None], (peers, *x.shape))  3.7 us
    sub x4, other arithmetic, complex_join(): real = upper[..., :width] - lower[..., width:]  3.27 us
  transfers between devices with their start and end apart: 4, of which 3 were waited for; matrix products, arithmetic and copies ran while one was open for 5% of the time, Pallas kernels for 22%

profile of v1, /device:TPU:8, one launch (start us, length us, event | category | flops | bytes accessed | tf_op | source)
XLA Modules:
  0.0 153.8 jit_solution(13818582508435976607)
XLA Ops:
  0.6 0.0 copy-start
  0.6 0.0 copy-start.3
  0.7 1.3 dynamic_slice.7
  1.9 0.6 fusion.8
  2.6 1.3 multiply_select_fusion
  3.9 0.8 multiply_convert_fusion.1.dens
  4.8 0.0 copy-start.1
  4.8 0.8 broadcast_in_dim.25
  5.6 5.8 %all-to-all-start.3 = ((bf16[16,32,512]{2,1,0:T(8,128)(2,1)}), bf16[16,32,512]{2,1,0:T(8,128)(2,1)S(1)}, u32[]{:S(2)}, u32[]{:S(2)}) async-start(bf16[16,32,512]{2,1,0:T(8,128)(2,1)} %broadcast_in_dim.25), calls=%async_computation.3 | async-start | bytes 1048576 | tf_op jit(solution)/shard_map/all_to_all | solution.py:139
  11.4 0.9 dynamic-slice_reduce_fusion
  12.3 0.8 subtract_multiply_fusion.1
  13.1 0.6 concatenate.27.tgt
  13.7 0.6 concatenate.25.src.tgt
  14.3 0.0 copy-done.1
  14.3 2.6 %shard_map.86 = f32[32,1024]{1,0:T(8,128)} custom-call(f32[8,512]{1,0:T(8,128)} %concatenate.27.tgt, f32[8,512]{1,0:T(8,128)} %concatenate.25.src.tgt, bf16[32,512]{1,0:T(8,128)(2,1)} %copy-done.1), custom_call_target="tpu_custom_call" | custom-call | tf_op jit(solution)/shard_map/pallas_call | solution.py:91
  16.9 0.8 slice_subtract_fusion.2
  17.7 4.5 %all-to-all-done.3 = bf16[16,32,512]{2,1,0:T(8,128)(2,1)S(1)} async-done(((bf16[16,32,512]{2,1,0:T(8,128)(2,1)}), bf16[16,32,512]{2,1,0:T(8,128)(2,1)S(1)}, u32[]{:S(2)}, u32[]{:S(2)}) %all-to-all-start.3) | async-done | bytes 524320 | tf_op jit(solution)/shard_map/all_to_all | solution.py:139
  22.2 1.1 broadcast_in_dim.19
  23.3 3.7 %all-to-all-start = ((f32[16,32,512]{2,1,0:T(8,128)}), f32[16,32,512]{2,1,0:T(8,128)S(1)}, u32[]{:S(2)}, u32[]{:S(2)}) async-start(f32[16,32,512]{2,1,0:T(8,128)} %broadcast_in_dim.19), calls=%async_computation | async-start | bytes 2097152 | tf_op jit(solution)/shard_map/all_to_all | solution.py:139
  27.0 16.5 %all-to-all-done = f32[16,32,512]{2,1,0:T(8,128)S(1)} async-done(((f32[16,32,512]{2,1,0:T(8,128)}), f32[16,32,512]{2,1,0:T(8,128)S(1)}, u32[]{:S(2)}, u32[]{:S(2)}) %all-to-all-start) | async-done | bytes 1048608 | tf_op jit(solution)/shard_map/all_to_all | solution.py:139
  43.5 0.9 broadcast_in_dim.24
  44.3 3.6 %all-to-all-start.2 = ((f32[16,16,512]{2,1,0:T(8,128)}), f32[16,16,512]{2,1,0:T(8,128)S(1)}, u32[]{:S(2)}, u32[]{:S(2)}) async-start(f32[16,16,512]{2,1,0:T(8,128)} %broadcast_in_dim.24), calls=%async_computation.2 | async-start | bytes 1048576 | tf_op jit(solution)/shard_map/all_to_all | solution.py:139
  47.9 0.1 reduce_sum.9
  48.0 0.0 copy-start.2
  48.0 10.7 %all-to-all-done.2 = f32[16,16,512]{2,1,0:T(8,128)S(1)} async-done(((f32[16,16,512]{2,1,0:T(8,128)}), f32[16,16,512]{2,1,0:T(8,128)S(1)}, u32[]{:S(2)}, u32[]{:S(2)}) %all-to-all-start.2) | async-done | bytes 524320 | tf_op jit(solution)/shard_map/all_to_all | solution.py:139
  58.7 0.9 broadcast_in_dim.23
  59.6 10.7 %all-to-all-start.1 = ((bf16[16,32,512]{2,1,0:T(8,128)(2,1)}), bf16[16,32,512]{2,1,0:T(8,128)(2,1)S(1)}, u32[]{:S(2)}, u32[]{:S(2)}) async-start(bf16[16,32,512]{2,1,0:T(8,128)(2,1)} %broadcast_in_dim.23), calls=%async_computation.1 | async-start | bytes 1048576 | tf_op jit(solution)/shard_map/all_to_all | solution.py:139
  70.2 1.0 subtract_multiply_fusion
  71.2 0.7 concatenate.26.src
  72.0 0.8 copy.16
  72.8 0.9 fusion.9
  73.7 32.0 %shard_map.88 = (f32[32,1024]{1,0:T(8,128)}, bf16[8192,1024]{1,0:T(8,128)(2,1)}) custom-call(f32[8,512]{1,0:T(8,128)} %concatenate.25.src.tgt, f32[8,8192]{1,0:T(8,128)} %bitcast.21, f32[8,8192]{1,0:T(8,128)} %bitcast.20, bf16[32,8192]{1,0:T(8,128)(2,1)} %bitcast.17), custom_call_target="tpu_custom_call" | custom-call | tf_op jit(solution)/shard_map/pallas_call | solution.py:132
  105.7 0.8 slice_subtract_fusion.3
  106.5 0.0 all-to-all-done.1
  106.5 0.9 broadcast_select_fusion.dens
  107.4 19.5 %shard_map.87 = f32[32,1024]{1,0:T(8,128)} custom-call(f32[8,512]{1,0:T(8,128)} %concatenate.25.src.tgt, f32[8,8192]{1,0:T(8,128)} %concatenate.26.src, bf16[32,8192]{1,0:T(8,128)(2,1)} %broadcast_select_fusion.dens), custom_call_target="tpu_custom_call" | custom-call | tf_op jit(solution)/shard_map/pallas_call | solution.py:91
  126.9 0.8 slice_subtract_fusion.1
  127.7 0.0 copy-done
  127.7 0.0 copy-done.3
  127.8 13.5 %all_to_all.25 = bf16[16,32,512]{2,1,0:T(8,128)(2,1)S(1)} all-to-all(bf16[16,32,512]{2,1,0:T(8,128)(2,1)S(1)} %broadcast_in_dim.26), channel_id=1, replica_groups=mesh['body'=16,'tile'=16] {'tile'}, dimensions={0} | all-to-all | bytes 1048576 | tf_op jit(solution)/shard_map/all_to_all | solution.py:139
  141.3 0.8 copy.17
  142.1 10.1 %shard_map.89 = f32[32,1024]{1,0:T(8,128)} custom-call(bf16[32,8192]{1,0:T(8,128)(2,1)} %bitcast.13, bf16[8192,1024]{1,0:T(8,128)(2,1)} %get-tuple-element.5.kin), custom_call_target="tpu_custom_call" | custom-call | tf_op jit(solution)/shard_map/pallas_call | solution.py:183
  152.3 0.8 slice_subtract_fusion
  153.1 0.7 fusion.3
  153.7 0.0 copy-done.2
  (8 shorter events, 0.2 us)
Async XLA Ops:
  0.6 127.1 %copy-start = (f32[32,512]{1,0:T(8,128)S(1)}, f32[32,512]{1,0:T(8,128)}, u32[]{:S(2)}) copy-start(f32[32,512]{1,0:T(8,128)} %param.12) | copy-start | bytes 196612
  0.6 127.1 %copy-start.3 = (f32[32,512]{1,0:T(8,128)S(1)}, f32[32,512]{1,0:T(8,128)}, u32[]{:S(2)}) copy-start(f32[32,512]{1,0:T(8,128)} %param.13) | copy-start | bytes 196612
  4.8 9.5 %copy-start.1 = (bf16[32,512]{1,0:T(8,128)(2,1)}, bf16[32,512]{1,0:T(8,128)(2,1)S(1)}, u32[]{:S(2)}) copy-start(bf16[32,512]{1,0:T(8,128)(2,1)S(1)} %multiply_convert_fusion.1.dens) | copy-start | bytes 98308
  5.6 16.6 %all-to-all-start.3 = ((bf16[16,32,512]{2,1,0:T(8,128)(2,1)}), bf16[16,32,512]{2,1,0:T(8,128)(2,1)S(1)}, u32[]{:S(2)}, u32[]{:S(2)}) async-start(bf16[16,32,512]{2,1,0:T(8,128)(2,1)} %broadcast_in_dim.25), calls=%async_computation.3 | async-start | bytes 1048576 | tf_op jit(solution)/shard_map/all_to_all | solution.py:139
  23.3 20.2 %all-to-all-start = ((f32[16,32,512]{2,1,0:T(8,128)}), f32[16,32,512]{2,1,0:T(8,128)S(1)}, u32[]{:S(2)}, u32[]{:S(2)}) async-start(f32[16,32,512]{2,1,0:T(8,128)} %broadcast_in_dim.19), calls=%async_computation | async-start | bytes 2097152 | tf_op jit(solution)/shard_map/all_to_all | solution.py:139
  44.3 14.4 %all-to-all-start.2 = ((f32[16,16,512]{2,1,0:T(8,128)}), f32[16,16,512]{2,1,0:T(8,128)S(1)}, u32[]{:S(2)}, u32[]{:S(2)}) async-start(f32[16,16,512]{2,1,0:T(8,128)} %broadcast_in_dim.24), calls=%async_computation.2 | async-start | bytes 1048576 | tf_op jit(solution)/shard_map/all_to_all | solution.py:139
  48.0 105.7 %copy-start.2 = (f32[32,512]{1,0:T(8,128)}, f32[32,512]{1,0:T(8,128)S(1)}, u32[]{:S(2)}) copy-start(f32[32,512]{1,0:T(8,128)S(1)} %reduce_sum.9) | copy-start | bytes 196612
  59.6 46.9 %all-to-all-start.1 = ((bf16[16,32,512]{2,1,0:T(8,128)(2,1)}), bf16[16,32,512]{2,1,0:T(8,128)(2,1)S(1)}, u32[]{:S(2)}, u32[]{:S(2)}) async-start(bf16[16,32,512]{2,1,0:T(8,128)(2,1)} %broadcast_in_dim.23), calls=%async_computation.1 | async-start | bytes 1048576 | tf_op jit(solution)/shard_map/all_to_all | solution.py:139

commit v2 on v1

v2 whole, which is shorter than its diff:
```python
import functools
import math

import jax
import jax.numpy as jnp
from jax import lax
from jax.experimental import pallas as pl
from jax.experimental.pallas import tpu as pltpu
from jax.sharding import PartitionSpec as P

KAPPA = 3.0/(2*math.pi)
S3=(4.442867903030504, -7.307443421264801, 3.5947880783718604, -0.7843740306771035)
BF=jnp.bfloat16; F32=jnp.float32

def pieces(v):
    h=v.astype(BF).astype(F32); r=v-h
    m=r.astype(BF).astype(F32)
    return h,m,r-m
def pick(rows,a,b,c,d,e,f):
    z=jnp.zeros_like(rows,dtype=F32)
    for k,v in enumerate((a,b,c,d,e,f)):
        z=jnp.where(rows==k,v,z)
    return z
def dot3(a,b):
    return jnp.broadcast_to(jnp.sum(a*b,axis=0,keepdims=True),a.shape)
def target_features(x):
    h,m,l=pieces(x); a,b,c=pieces(dot3(x,x))
    rows=lax.broadcasted_iota(jnp.int32,x.shape,0)
    tail=pick(rows,a,b,c,1.0,1.0,1.0)
    return jnp.concatenate([h,h,h,m,m,l,tail,jnp.zeros_like(tail)],0).astype(BF)
def source_features(y):
    h,m,l=pieces(-2.0*y); a,b,c=pieces(dot3(y,y)+0.01*KAPPA*KAPPA)
    rows=lax.broadcasted_iota(jnp.int32,y.shape,0)
    tail=pick(rows,1.0,1.0,1.0,a,b,c)
    return jnp.concatenate([h,m,l,h,m,h,tail,jnp.zeros_like(tail)],0).astype(BF)
def normal_features(n,y):
    h,m,l=pieces(n); a,b,c=pieces(-dot3(n,y))
    rows=lax.broadcasted_iota(jnp.int32,y.shape,0)
    tail=pick(rows,0.0,0.0,0.0,a,b,c)
    return jnp.concatenate([h,m,l,h,m,h,tail,jnp.zeros_like(tail)],0).astype(BF)
def cross(a,b):
    return lax.dot_general(a,b,(((0,),(0,)),((),())),preferred_element_type=F32)
def wave(u):
    inv=lax.rsqrt(u); turn=u*inv
    f=turn-jnp.round(turn); z=f*f
    s=f*(((S3[3]*z+S3[2])*z+S3[1])*z+S3[0])
    q=s*s
    b=2.0-q
    return inv,1.0-q,s*(b*lax.rsqrt(b))
def point_values(u):
    inv,c,s=wave(u)
    return (c*inv).astype(BF),(s*inv).astype(BF)
def layer_values(u,p):
    inv,c,s=wave(u)
    e=p*(inv*inv); g=inv+e; h=e*(inv*(1/(2*math.pi)))
    return (c*h+s*g).astype(BF),(s*h-c*g).astype(BF)


N = 16
ROWS = 512
HALF = 256
OWNERS = 8
FIRST = 7
KEPT = 10
STEP = 16
MESH = pl.DeviceIdType.MESH


def join(raw):
    return jnp.concatenate(
        [raw[:16, :ROWS] - raw[16:, ROWS:], raw[:16, ROWS:] + raw[16:, :ROWS]], 0
    )


def sweep_kernel(
    counts, points, normals, weights, sources, dens, inc, out, amp_out,
    geo, spots, fst, feat, ubuf, pbuf, kbuf, acc, kst, gbuf, dbuf, d1buf, abuf, part, rbuf, ampf, tile,
    sfeat, afeat, nfeat, g_s, g_r, d_s, d_r, r_s, r_r, f_s, f_r, b_s, b_r, w_s, w_r, s_s, s_r,
):
    me = lax.axis_index("tile")
    group = lax.axis_index("body")

    def send(source, target, ssem, rsem, where):
        return pltpu.make_async_remote_copy(
            src_ref=source, dst_ref=target, send_sem=ssem, recv_sem=rsem,
            device_id=where, device_id_type=MESH,
        )

    barrier = pltpu.get_barrier_semaphore()

    @pl.loop(1, N)
    def _(k):
        pl.semaphore_signal(barrier, inc=1, device_id={"tile": (me + k) % N}, device_id_type=MESH)
        pl.semaphore_signal(barrier, inc=1, device_id={"body": (group + k) % N}, device_id_type=MESH)

    rows8 = lax.broadcasted_iota(jnp.int32, (8, HALF), 0)

    def only(x, first):
        if first:
            x = pltpu.roll(x, 8 - first, 0)
        return jnp.where(rows8 < 3, x, 0.0)

    def columns(i):
        return pl.ds(pl.multiple_of(i * HALF, HALF), HALF)

    first = pl.ds(pl.multiple_of(group * ROWS, ROWS), 128)
    centre = sources[:, first][:, 0:1]
    slot_of = me * ROWS + lax.broadcasted_iota(jnp.int32, (1, ROWS), 1)
    live = jnp.where(slot_of < counts[group], 1.0, 0.0)
    scale = KAPPA * weights[...] * live
    geo[0:3, :] = KAPPA * (points[...] - centre)
    geo[3:6, :] = 3.0 * normals[...]
    geo[6:8, :] = jnp.zeros((2, ROWS), F32)
    spots[...] = jnp.zeros_like(spots)
    spots[0:3, :] = KAPPA * (sources[...] - centre)
    sigma0 = dens[...] * live

    def loaded(sigma):
        return (scale * sigma.astype(BF).astype(F32)).astype(BF)

    dbuf[me] = loaded(sigma0)

    def load_targets(part_of):
        for th in range(2):
            feat[:, th * HALF:(th + 1) * HALF] = target_features(only(part_of(th), 0))

    def fill_point(a, slot):
        for th in range(2):
            c = slice(th * HALF, (th + 1) * HALF)
            ubuf[slot, :, c] = jnp.dot(a, feat[:, c], preferred_element_type=F32)

    def evaluate_point(slot, into):
        for th in range(2):
            for ch in range(HALF // STEP):
                r = slice(ch * STEP, (ch + 1) * STEP)
                re, im = point_values(ubuf[slot, r, th * HALF:(th + 1) * HALF])
                into[slot, r, th * HALF:(th + 1) * HALF] = re
                into[slot, r, ROWS + th * HALF:ROWS + (th + 1) * HALF] = im

    def flip(x):
        return jnp.transpose(x)

    @pl.loop(0, 2 * N)
    def _(i):
        sfeat[columns(i), :] = flip(source_features(spots[:, columns(i)]))

    load_targets(lambda th: spots[:, columns(2 * group + th)])
    for h in range(2):
        fill_point(flip(source_features(only(geo[:, h * HALF:(h + 1) * HALF], 0))), h)
    for h in range(2):
        evaluate_point(h, kbuf)
    raw = jnp.dot(dbuf[me, :, :HALF], kbuf[0], preferred_element_type=F32)
    raw += jnp.dot(dbuf[me, :, HALF:], kbuf[1], preferred_element_type=F32)
    part[...] = join(raw)

    def geo_copy(k):
        return send(geo, gbuf.at[me], g_s.at[k], g_r.at[k], {"tile": (me + N - k) % N})

    def dens_copy(k):
        return send(dbuf.at[me], dbuf.at[me], d_s.at[k], d_r.at[k], {"tile": (me + N - k) % N})

    def spot(t):
        return (
            pl.ds(pl.multiple_of((t // 4) * 16, 16), 16),
            pl.ds(pl.multiple_of((t % 4) * 128, 128), 128),
        )

    def reduce_copy(k):
        peer = (me + k) % N
        at = spot(peer // 2)
        return send(part.at[at[0], at[1]], rbuf.at[k], r_s.at[k], r_r.at[k], {"tile": peer})

    gbuf[me] = geo[...]
    load_targets(lambda th: geo[:, th * HALF:(th + 1) * HALF])

    def fill_field(m, h, slot):
        other = (group + 1 + m) % N
        fill_point(sfeat[columns(2 * other + h), :], slot)

    def begin():
        pl.semaphore_wait(barrier, 2 * (N - 1))

        @pl.loop(1, N)
        def _(k):
            geo_copy(k).start()
            dens_copy(k).start()

            @pl.when((me + k) % 2 == 0)
            def _():
                reduce_copy(k).start()

    fill_field(0, 0, 0)

    @pl.loop(0, KEPT)
    def _(m):
        @pl.when(m == FIRST)
        def _():
            begin()

        fill_field(m, 1, 1)
        evaluate_point(0, fst.at[m])
        fill_field((m + 1) % (N - 1), 0, 0)
        evaluate_point(1, fst.at[m])

    def full_copy(k):
        at = spot(me // 2)
        return send(tile, ampf.at[at[0], at[1]], f_s.at[k], f_r.at[me // 2], {"tile": (me + k) % N})

    def body_copy(k):
        at = spot(me // 2)
        here = abuf.at[group, at[0], at[1]]
        return send(here, here, b_s.at[k], b_r.at[k], {"body": (group + k) % N})

    def spread_copy(k):
        at = spot(me // 2)
        here = abuf.at[:, at[0], at[1]]
        return send(here, here, w_s.at[k], w_r.at[me // 2], {"tile": (me + k) % N})

    def finish_amplitudes():
        @pl.when(me % 2 == 0)
        def _():
            at = spot(me // 2)

            @pl.loop(1, N)
            def _(k):
                reduce_copy(k).wait_recv()

            total = part[at[0], at[1]]
            for k in range(1, N):
                total = total + rbuf[k]
            tile[...] = total
            ampf[at[0], at[1]] = total
            abuf[group, at[0], at[1]] = total.astype(BF)

            @pl.loop(1, N)
            def _(k):
                body_copy(k).start()
                full_copy(k).start()

    def spread_amplitudes():
        @pl.when(me % 2 == 0)
        def _():
            @pl.loop(1, N)
            def _(k):
                body_copy(k).wait_recv()

            @pl.loop(1, N)
            def _(k):
                spread_copy(k).start()

    def prepare(j, p):
        for h in range(2):
            c = slice(h * HALF, (h + 1) * HALF)
            g = gbuf[j, :, c]
            y = only(g, 0)
            afeat[p, c, :] = flip(source_features(y))
            nfeat[p, c, :] = flip(normal_features(only(g, 3), y))

    def fill_layer(p, h, slot):
        r = slice(h * HALF, (h + 1) * HALF)
        for th in range(2):
            c = slice(th * HALF, (th + 1) * HALF)
            ubuf[slot, :, c] = jnp.dot(afeat[p, r, :], feat[:, c], preferred_element_type=F32)
            pbuf[slot, :, c] = jnp.dot(nfeat[p, r, :], feat[:, c], preferred_element_type=F32)

    def evaluate_layer(j, h):
        for th in range(2):
            for ch in range(HALF // STEP):
                at = (h, slice(ch * STEP, (ch + 1) * STEP), slice(th * HALF, (th + 1) * HALF))
                re, im = layer_values(ubuf[at], pbuf[at])
                r = slice(h * HALF + ch * STEP, h * HALF + (ch + 1) * STEP)
                kst[j, r, th * HALF:(th + 1) * HALF] = re
                kst[j, r, ROWS + th * HALF:ROWS + (th + 1) * HALF] = im
                kbuf[h, at[1], th * HALF:(th + 1) * HALF] = re
                kbuf[h, at[1], ROWS + th * HALF:ROWS + (th + 1) * HALF] = im

    def contract_layer(j, h):
        c = slice(h * HALF, (h + 1) * HALF)
        acc[...] += jnp.dot(dbuf[j, :, c], kbuf[h], preferred_element_type=F32)

    acc[...] = jnp.zeros_like(acc)
    kbuf[1] = jnp.zeros((HALF, 2 * ROWS), BF)
    prepare(me, 0)
    fill_layer(0, 0, 0)

    @pl.loop(0, N)
    def _(k):
        p = k % 2
        j = (me + k) % N
        before = (me + k - (k + N - 2) // (N - 1)) % N
        after = (me + k + 1) % N

        @pl.when(k == 3)
        def _():
            finish_amplitudes()

        @pl.when(k == 9)
        def _():
            spread_amplitudes()

        @pl.when(k < N - 1)
        def _():
            geo_copy(k + 1).wait_recv()
            dens_copy(k + 1).wait_recv()

        prepare(after, 1 - p)
        fill_layer(p, 1, 1)
        evaluate_layer(j, 0)
        contract_layer(before, 1)
        fill_layer(1 - p, 0, 0)
        evaluate_layer(j, 1)
        contract_layer(j, 0)

    contract_layer((me + N - 1) % N, 1)
    image = join(acc[...])

    @pl.loop(0, OWNERS)
    def _(o):
        @pl.when(2 * o != me)
        def _():
            at = spot(o)
            here = abuf.at[:, at[0], at[1]]
            send(here, here, w_s.at[0], w_r.at[o], {"tile": (me + 1) % N}).wait_recv()

    acc[...] = jnp.zeros_like(acc)
    kbuf[1] = jnp.zeros((HALF, 2 * ROWS), BF)

    def contract_field(m, h):
        other = (group + 1 + m) % N
        acc[...] += jnp.dot(
            abuf[other, :, h * HALF:(h + 1) * HALF], kbuf[h], preferred_element_type=F32
        )

    fill_field(KEPT, 0, 0)

    @pl.loop(KEPT, N - 1)
    def _(m):
        fill_field(m, 1, 1)
        evaluate_point(0, kbuf)
        contract_field(m - (m - KEPT + N - 2) // (N - 1), 1)
        fill_field((m + 1) % (N - 1), 0, 0)
        evaluate_point(1, kbuf)
        contract_field(m, 0)

    contract_field(N - 2, 1)

    @pl.loop(0, KEPT)
    def _(m):
        other = (group + 1 + m) % N
        for h in range(2):
            acc[...] += jnp.dot(
                abuf[other, :, h * HALF:(h + 1) * HALF], fst[m, h], preferred_element_type=F32
            )

    rhs = live * (inc[...] - KAPPA * join(acc[...]))
    sigma = live * (sigma0 + rhs - 0.5 * sigma0 - image)
    d1buf[me] = loaded(sigma)

    def next_copy(k):
        return send(d1buf.at[me], d1buf.at[me], s_s.at[k], s_r.at[k], {"tile": (me + N - k) % N})

    @pl.loop(1, N)
    def _(k):
        next_copy(k).start()

    acc[...] = jnp.dot(d1buf[me], kst[me], preferred_element_type=F32)

    @pl.loop(1, N)
    def _(k):
        j = (me + k) % N
        next_copy(k).wait_recv()
        acc[...] += jnp.dot(d1buf[j], kst[j], preferred_element_type=F32)

    out[...] = live * (sigma + rhs - 0.5 * sigma - join(acc[...]))

    @pl.loop(0, OWNERS)
    def _(o):
        @pl.when(2 * o != me)
        def _():
            at = spot(o)
            send(tile, ampf.at[at[0], at[1]], f_s.at[0], f_r.at[o], {"tile": (me + 1) % N}).wait_recv()

    amp_out[...] = ampf[...]

    @pl.loop(1, N)
    def _(k):
        geo_copy(k).wait_send()
        dens_copy(k).wait_send()
        next_copy(k).wait_send()

        @pl.when((me + k) % 2 == 0)
        def _():
            reduce_copy(k).wait_send()

        @pl.when(me % 2 == 0)
        def _():
            body_copy(k).wait_send()
            full_copy(k).wait_send()
            spread_copy(k).wait_send()


def per_device(panel_points, normals, weights, counts, source_points, density, incident):
    channels, rows = density.shape
    per_body = source_points.shape[1] // lax.axis_size("body")
    V = pltpu.VMEM
    D = pltpu.SemaphoreType.DMA
    wide = 2 * rows
    return pl.pallas_call(
        sweep_kernel,
        out_shape=(
            jax.ShapeDtypeStruct((channels, rows), F32),
            jax.ShapeDtypeStruct((channels, per_body), F32),
        ),
        in_specs=[pl.BlockSpec(memory_space=pltpu.SMEM)]
        + [pl.BlockSpec(memory_space=pltpu.VMEM)] * 6,
        out_specs=(pl.BlockSpec(memory_space=pltpu.VMEM),) * 2,
        scratch_shapes=[
            V((8, rows), F32),
            V((8, N * rows), F32),
            V((KEPT, 2, HALF, wide), BF),
            V((64, rows), BF),
            V((2, HALF, rows), F32),
            V((2, HALF, rows), F32),
            V((2, HALF, wide), BF),
            V((channels, wide), F32),
            V((N, rows, wide), BF),
            V((N, 8, rows), F32),
            V((N, channels, rows), BF),
            V((N, channels, rows), BF),
            V((N, channels, per_body), BF),
            V((channels, per_body), F32),
            V((N, 16, 128), F32),
            V((channels, per_body), F32),
            V((16, 128), F32),
            V((N * rows, 64), BF),
            V((2, rows, 64), BF),
            V((2, rows, 64), BF),
        ]
        + [D((N,))] * 14,
        compiler_params=pltpu.CompilerParams(
            collective_id=0, has_side_effects=True, vmem_limit_bytes=60 * 2**20
        ),
    )(counts, panel_points, normals, weights[None], source_points, density, incident)


def solution(mesh):
    in_specs = (
        P(None, ("body", "tile")),
        P(None, ("body", "tile")),
        P(("body", "tile")),
        P(),
        P(),
        P(None, ("body", "tile")),
        P(None, ("body", "tile")),
    )
    out_specs = (P(None, ("body", "tile")), P(None, "body"))
    return jax.shard_map(
        per_device, mesh=mesh, in_specs=in_specs, out_specs=out_specs, check_vma=False
    )
```

time: 155 us -> 72 us (0.46)
  waiting for transfers between devices: 31.7 us -> 0 us
  starting transfers between devices: 23.6 us -> 0 us
  blocking collectives: 13.5 us -> 0 us
  other arithmetic: 9.58 us -> 0 us
  local copies, waits for them, and re-layouts: 10.4 us -> 2.14 us
  Pallas kernels: 64.2 us -> 67.9 us
    all_to_all x4 -> x0, waiting for transfers between devices: 31.7 us -> none  [copy_for_each(): lax.all_to_all(jnp.broadcast_to(x[None], (peers, *x.shape)), axis, 0, 0,...]
    all_to_all x4 -> x0, starting transfers between devices: 23.6 us -> none  [copy_for_each(): lax.all_to_all(jnp.broadcast_to(x[None], (peers, *x.shape)), axis, 0, 0,...]
    all_to_all x1 -> x0, blocking collectives: 13.5 us -> none  [copy_for_each(): lax.all_to_all(jnp.broadcast_to(x[None], (peers, *x.shape)), axis, 0, 0,...]
    mul x4 -> x0, other arithmetic: 3.81 us -> none  [the longest x1 1.33 us: per_device(): scale = KAPPA * weights * live]
    pallas_call x4 -> x1, Pallas kernels: 64.2 us -> 67.9 us  [per_device(): pl.pallas_call(sweep_kernel, out_shape=(jax.ShapeDtypeStruct((channels, r...]
    broadcast_in_dim x5 -> x0, local copies, waits for them, and re-layouts: 3.7 us -> none  [copy_for_each(): jnp.broadcast_to(x[None], (peers, *x.shape))]
    sub x4 -> x0, other arithmetic: 3.27 us -> none  [complex_join(): real = upper[..., :width] - lower[..., width:]]
    unnamed x8 -> x4, local copies, waits for them, and re-layouts: 0.02 us -> 2.14 us
  transfers between devices with their start and end apart: 4 -> 0, of which waited for: 3 -> 0; matrix products, arithmetic and copies ran while one was open for 5% -> 0% of each run, Pallas kernels for 22% -> 0%
where the time goes in v2:
time: 72 us; the launch traced here: 70.7 us
  Pallas kernels  67.9 us (94%)
  local copies, waits for them, and re-layouts  2.14 us (3%)
    pallas_call x1, Pallas kernels, per_device(): pl.pallas_call(sweep_kernel, out_shape=(jax.ShapeDtypeStruct((channels, r...  67.9 us
    unnamed x4, local copies, waits for them, and re-layouts  2.14 us

profile of v2, /device:TPU:8, one launch (start us, length us, event | category | flops | bytes accessed | tf_op | source)
XLA Modules:
  0.0 70.7 jit_solution(6525523709377767808)
XLA Ops:
  0.6 67.9 %shard_map.86 = (f32[32,512]{1,0:T(8,128)}, f32[32,512]{1,0:T(8,128)}) custom-call(s32[16]{0:T(128)} %counts.1, f32[3,512]{1,0:T(4,128)} %points.1, f32[3,512]{1,0:T(4,128)} %normals.1, f32[1,512]{1,0:T(1,128)} %bitcast.1, f32[3,8192]{1,0:T(4,128)} %sources.1, f32[32,512]{1,0:T(8,128)} %dens.1, f32[32,512]{1,0:T(8,128)} %inc.1), custom_call_target="tpu_custom_call" | custom-call | tf_op jit(solution)/shard_map/pallas_call | solution.py:408
  68.6 0.0 copy-start
  68.6 1.5 %copy.11 = f32[32,512]{1,0:T(8,128)} copy(f32[32,512]{1,0:T(8,128)} %get-tuple-element.4) | data formatting | bytes 131072
  70.1 0.0 copy-done
  70.1 0.6 copy.12
Async XLA Ops:
  68.6 1.5 %copy-start = (f32[32,512]{1,0:T(8,128)S(1)}, f32[32,512]{1,0:T(8,128)}, u32[]{:S(2)}) copy-start(f32[32,512]{1,0:T(8,128)} %get-tuple-element.5) | copy-start | bytes 196612

commit v3 on v2

--- a/solution.py
+++ b/solution.py
@@ -60,8 +60,8 @@
 ROWS = 512
 HALF = 256
 OWNERS = 8
-FIRST = 7
-KEPT = 10
+FIRST = 6
+KEPT = 15
 STEP = 16
 MESH = pl.DeviceIdType.MESH
 
@@ -153,11 +153,22 @@
     raw += jnp.dot(dbuf[me, :, HALF:], kbuf[1], preferred_element_type=F32)
     part[...] = join(raw)
 
-    def geo_copy(k):
-        return send(geo, gbuf.at[me], g_s.at[k], g_r.at[k], {"tile": (me + N - k) % N})
-
-    def dens_copy(k):
-        return send(dbuf.at[me], dbuf.at[me], d_s.at[k], d_r.at[k], {"tile": (me + N - k) % N})
+    partner = me + 1 - 2 * (me % 2)
+    chips = N // 2
+
+    def to_chip(ref, ss, rs, d):
+        own = ref.at[me]
+        return send(own, own, ss.at[d], rs.at[d], {"tile": (me + N - 2 * d) % N})
+
+    def to_partner(ref, ss, rs):
+        own = ref.at[me]
+        return send(own, own, ss.at[chips], rs.at[chips], {"tile": partner})
+
+    def relay(ref, ss, rs, d):
+        got = ref.at[(me + 2 * d) % N]
+        return send(got, got, ss.at[chips + d], rs.at[chips + d], {"tile": partner})
+
+    panels = ((gbuf, g_s, g_r), (dbuf, d_s, d_r))
 
     def spot(t):
         return (
@@ -180,11 +191,14 @@
     def begin():
         pl.semaphore_wait(barrier, 2 * (N - 1))
 
+        for buffers in panels:
+            to_partner(*buffers).start()
+        for d in (1, 2):
+            for buffers in panels:
+                to_chip(*buffers, d).start()
+
         @pl.loop(1, N)
         def _(k):
-            geo_copy(k).start()
-            dens_copy(k).start()
-
             @pl.when((me + k) % 2 == 0)
             def _():
                 reduce_copy(k).start()
@@ -207,13 +221,11 @@
         return send(tile, ampf.at[at[0], at[1]], f_s.at[k], f_r.at[me // 2], {"tile": (me + k) % N})
 
     def body_copy(k):
-        at = spot(me // 2)
-        here = abuf.at[group, at[0], at[1]]
+        here = abuf.at[me // 2, group]
         return send(here, here, b_s.at[k], b_r.at[k], {"body": (group + k) % N})
 
     def spread_copy(k):
-        at = spot(me // 2)
-        here = abuf.at[:, at[0], at[1]]
+        here = abuf.at[me // 2]
         return send(here, here, w_s.at[k], w_r.at[me // 2], {"tile": (me + k) % N})
 
     def finish_amplitudes():
@@ -230,7 +242,7 @@
                 total = total + rbuf[k]
             tile[...] = total
             ampf[at[0], at[1]] = total
-            abuf[group, at[0], at[1]] = total.astype(BF)
+            abuf[me // 2, group] = total.astype(BF)
 
             @pl.loop(1, N)
             def _(k):
@@ -248,128 +260,138 @@
             def _(k):
                 spread_copy(k).start()
 
-    def prepare(j, p):
-        for h in range(2):
-            c = slice(h * HALF, (h + 1) * HALF)
-            g = gbuf[j, :, c]
-            y = only(g, 0)
-            afeat[p, c, :] = flip(source_features(y))
-            nfeat[p, c, :] = flip(normal_features(only(g, 3), y))
-
-    def fill_layer(p, h, slot):
-        r = slice(h * HALF, (h + 1) * HALF)
+    def prepare(j, h):
+        g = gbuf[j, :, h * HALF:(h + 1) * HALF]
+        y = only(g, 0)
+        afeat[h] = flip(source_features(y))
+        nfeat[h] = flip(normal_features(only(g, 3), y))
+
+    def fill_layer(h):
         for th in range(2):
             c = slice(th * HALF, (th + 1) * HALF)
-            ubuf[slot, :, c] = jnp.dot(afeat[p, r, :], feat[:, c], preferred_element_type=F32)
-            pbuf[slot, :, c] = jnp.dot(nfeat[p, r, :], feat[:, c], preferred_element_type=F32)
+            ubuf[h, :, c] = jnp.dot(afeat[h], feat[:, c], preferred_element_type=F32)
+            pbuf[h, :, c] = jnp.dot(nfeat[h], feat[:, c], preferred_element_type=F32)
 
     def evaluate_layer(j, h):
         for th in range(2):
             for ch in range(HALF // STEP):
-                at = (h, slice(ch * STEP, (ch + 1) * STEP), slice(th * HALF, (th + 1) * HALF))
-                re, im = layer_values(ubuf[at], pbuf[at])
+                a = slice(ch * STEP, (ch + 1) * STEP)
+                c = slice(th * HALF, (th + 1) * HALF)
+                d = slice(ROWS + th * HALF, ROWS + (th + 1) * HALF)
+                re, im = layer_values(ubuf[h, a, c], pbuf[h, a, c])
                 r = slice(h * HALF + ch * STEP, h * HALF + (ch + 1) * STEP)
-                kst[j, r, th * HALF:(th + 1) * HALF] = re
-                kst[j, r, ROWS + th * HALF:ROWS + (th + 1) * HALF] = im
-                kbuf[h, at[1], th * HALF:(th + 1) * HALF] = re
-                kbuf[h, at[1], ROWS + th * HALF:ROWS + (th + 1) * HALF] = im
+                kst[j, r, c] = re
+                kst[j, r, d] = im
+                kbuf[h, a, c] = re
+                kbuf[h, a, d] = im
 
     def contract_layer(j, h):
-        c = slice(h * HALF, (h + 1) * HALF)
-        acc[...] += jnp.dot(dbuf[j, :, c], kbuf[h], preferred_element_type=F32)
+        acc[...] += jnp.dot(
+            dbuf[j, :, h * HALF:(h + 1) * HALF], kbuf[h], preferred_element_type=F32
+        )
 
     acc[...] = jnp.zeros_like(acc)
     kbuf[1] = jnp.zeros((HALF, 2 * ROWS), BF)
     prepare(me, 0)
-    fill_layer(0, 0, 0)
-
-    @pl.loop(0, N)
-    def _(k):
-        p = k % 2
-        j = (me + k) % N
-        before = (me + k - (k + N - 2) // (N - 1)) % N
-        after = (me + k + 1) % N
-
-        @pl.when(k == 3)
+    prepare(me, 1)
+    fill_layer(0)
+
+    @pl.loop(0, chips)
+    def _(pair):
+        some = (pair + chips - 1) // chips
+        before = (1 - some) * me + some * ((partner + 2 * pair + N - 2) % N)
+        here = ((me + 2 * pair) % N, (partner + 2 * pair) % N, (me + 2 * pair + 2) % N)
+
+        @pl.when(pair == 0)
         def _():
             finish_amplitudes()
 
-        @pl.when(k == 9)
+        @pl.when(pair == 5)
         def _():
             spread_amplitudes()
 
-        @pl.when(k < N - 1)
-        def _():
-            geo_copy(k + 1).wait_recv()
-            dens_copy(k + 1).wait_recv()
-
-        prepare(after, 1 - p)
-        fill_layer(p, 1, 1)
-        evaluate_layer(j, 0)
-        contract_layer(before, 1)
-        fill_layer(1 - p, 0, 0)
-        evaluate_layer(j, 1)
-        contract_layer(j, 0)
-
-    contract_layer((me + N - 1) % N, 1)
+        @pl.when(pair < chips - 3)
+        def _():
+            for buffers in panels:
+                to_chip(*buffers, pair + 3).start()
+
+        @pl.when(pair < chips - 1)
+        def _():
+            for buffers in panels:
+                to_chip(*buffers, pair + 1).wait_recv()
+                relay(*buffers, pair + 1).start()
+
+        @pl.when(pair == 0)
+        def _():
+            for buffers in panels:
+                to_partner(*buffers).wait_recv()
+
+        @pl.when(pair > 0)
+        def _():
+            for buffers in panels:
+                relay(*buffers, pair).wait_recv()
+
+        for t in range(4):
+            h = t % 2
+            fill_layer(1 - h)
+            evaluate_layer(here[t // 2], h)
+            prepare(here[t // 2 + 1], h)
+            contract_layer(before if t == 0 else here[(t - 1) // 2], 1 - h)
+
+    contract_layer((partner + N - 2) % N, 1)
     image = join(acc[...])
 
     @pl.loop(0, OWNERS)
     def _(o):
         @pl.when(2 * o != me)
         def _():
-            at = spot(o)
-            here = abuf.at[:, at[0], at[1]]
+            here = abuf.at[o]
             send(here, here, w_s.at[0], w_r.at[o], {"tile": (me + 1) % N}).wait_recv()
 
     acc[...] = jnp.zeros_like(acc)
-    kbuf[1] = jnp.zeros((HALF, 2 * ROWS), BF)
-
-    def contract_field(m, h):
-        other = (group + 1 + m) % N
-        acc[...] += jnp.dot(
-            abuf[other, :, h * HALF:(h + 1) * HALF], kbuf[h], preferred_element_type=F32
-        )
-
-    fill_field(KEPT, 0, 0)
-
-    @pl.loop(KEPT, N - 1)
-    def _(m):
-        fill_field(m, 1, 1)
-        evaluate_point(0, kbuf)
-        contract_field(m - (m - KEPT + N - 2) // (N - 1), 1)
-        fill_field((m + 1) % (N - 1), 0, 0)
-        evaluate_point(1, kbuf)
-        contract_field(m, 0)
-
-    contract_field(N - 2, 1)
+    def far(other, h):
+        rows = [
+            jnp.concatenate([abuf[c + 2 * h, other], abuf[c + 2 * h + 1, other]], 1)
+            for c in (0, 4)
+        ]
+        return jnp.concatenate(rows, 0)
 
     @pl.loop(0, KEPT)
     def _(m):
         other = (group + 1 + m) % N
-        for h in range(2):
-            acc[...] += jnp.dot(
-                abuf[other, :, h * HALF:(h + 1) * HALF], fst[m, h], preferred_element_type=F32
-            )
+        raw = jnp.dot(far(other, 0), fst[m, 0], preferred_element_type=F32)
+        raw += jnp.dot(far(other, 1), fst[m, 1], preferred_element_type=F32)
+        acc[...] += raw
 
     rhs = live * (inc[...] - KAPPA * join(acc[...]))
     sigma = live * (sigma0 + rhs - 0.5 * sigma0 - image)
     d1buf[me] = loaded(sigma)
 
-    def next_copy(k):
-        return send(d1buf.at[me], d1buf.at[me], s_s.at[k], s_r.at[k], {"tile": (me + N - k) % N})
-
-    @pl.loop(1, N)
-    def _(k):
-        next_copy(k).start()
-
+    update = (d1buf, s_s, s_r)
+
+    @pl.loop(1, chips)
+    def _(d):
+        to_chip(*update, d).start()
+
+    to_partner(*update).start()
     acc[...] = jnp.dot(d1buf[me], kst[me], preferred_element_type=F32)
 
-    @pl.loop(1, N)
-    def _(k):
-        j = (me + k) % N
-        next_copy(k).wait_recv()
+    def apply(j):
         acc[...] += jnp.dot(d1buf[j], kst[j], preferred_element_type=F32)
+
+    to_partner(*update).wait_recv()
+    apply(partner)
+
+    @pl.loop(1, chips)
+    def _(d):
+        to_chip(*update, d).wait_recv()
+        relay(*update, d).start()
+        apply((me + 2 * d) % N)
+
+    @pl.loop(1, chips)
+    def _(d):
+        relay(*update, d).wait_recv()
+        apply((partner + 2 * d) % N)
 
     out[...] = live * (sigma + rhs - 0.5 * sigma - join(acc[...]))
 
@@ -382,12 +404,16 @@
 
     amp_out[...] = ampf[...]
 
+    for buffers in panels + (update,):
+        to_partner(*buffers).wait_send()
+
+        @pl.loop(1, chips)
+        def _(d):
+            to_chip(*buffers, d).wait_send()
+            relay(*buffers, d).wait_send()
+
     @pl.loop(1, N)
     def _(k):
-        geo_copy(k).wait_send()
-        dens_copy(k).wait_send()
-        next_copy(k).wait_send()
-
         @pl.when((me + k) % 2 == 0)
         def _():
             reduce_copy(k).wait_send()
@@ -427,14 +453,14 @@
             V((N, 8, rows), F32),
             V((N, channels, rows), BF),
             V((N, channels, rows), BF),
-            V((N, channels, per_body), BF),
+            V((OWNERS, N, 16, 128), BF),
             V((channels, per_body), F32),
             V((N, 16, 128), F32),
             V((channels, per_body), F32),
             V((16, 128), F32),
             V((N * rows, 64), BF),
-            V((2, rows, 64), BF),
-            V((2, rows, 64), BF),
+            V((2, HALF, 64), BF),
+            V((2, HALF, 64), BF),
         ]
         + [D((N,))] * 14,
         compiler_params=pltpu.CompilerParams(

time: 72 us -> 66.2 us (0.919)
  Pallas kernels: 67.9 us -> 62.2 us
    pallas_call x1, Pallas kernels: 67.9 us -> 62.2 us  [per_device(): pl.pallas_call(sweep_kernel, out_shape=(jax.ShapeDtypeStruct((channels, r...]
where the time goes in v3:
time: 66.2 us; the launch traced here: 65 us
  Pallas kernels  62.2 us (94%)
  local copies, waits for them, and re-layouts  2.14 us (3%)
    pallas_call x1, Pallas kernels, per_device(): pl.pallas_call(sweep_kernel, out_shape=(jax.ShapeDtypeStruct((channels, r...  62.2 us
    unnamed x4, local copies, waits for them, and re-layouts  2.14 us

profile of v3, /device:TPU:8, one launch (start us, length us, event | category | flops | bytes accessed | tf_op | source)
XLA Modules:
  0.0 65.0 jit_solution(4771676881035499739)
XLA Ops:
  0.6 62.2 %shard_map.86 = (f32[32,512]{1,0:T(8,128)}, f32[32,512]{1,0:T(8,128)}) custom-call(s32[16]{0:T(128)} %counts.1, f32[3,512]{1,0:T(4,128)} %points.1, f32[3,512]{1,0:T(4,128)} %normals.1, f32[1,512]{1,0:T(1,128)} %bitcast.1, f32[3,8192]{1,0:T(4,128)} %sources.1, f32[32,512]{1,0:T(8,128)} %dens.1, f32[32,512]{1,0:T(8,128)} %inc.1), custom_call_target="tpu_custom_call" | custom-call | tf_op jit(solution)/shard_map/pallas_call | solution.py:434
  62.8 0.0 copy-start
  62.8 1.5 %copy.11 = f32[32,512]{1,0:T(8,128)} copy(f32[32,512]{1,0:T(8,128)} %get-tuple-element.4) | data formatting | bytes 131072
  64.3 0.0 copy-done
  64.4 0.6 copy.12
Async XLA Ops:
  62.8 1.5 %copy-start = (f32[32,512]{1,0:T(8,128)S(1)}, f32[32,512]{1,0:T(8,128)}, u32[]{:S(2)}) copy-start(f32[32,512]{1,0:T(8,128)} %get-tuple-element.5) | copy-start | bytes 196612

commit v4 on v3

--- a/solution.py
+++ b/solution.py
@@ -60,7 +60,8 @@
 ROWS = 512
 HALF = 256
 OWNERS = 8
-FIRST = 6
+FIRST = 5
+EARLY = 10
 KEPT = 15
 STEP = 16
 MESH = pl.DeviceIdType.MESH
@@ -149,8 +150,8 @@
         fill_point(flip(source_features(only(geo[:, h * HALF:(h + 1) * HALF], 0))), h)
     for h in range(2):
         evaluate_point(h, kbuf)
-    raw = jnp.dot(dbuf[me, :, :HALF], kbuf[0], preferred_element_type=F32)
-    raw += jnp.dot(dbuf[me, :, HALF:], kbuf[1], preferred_element_type=F32)
+    raw = jnp.dot(dbuf[me, :, :HALF], kbuf[0, :, :2 * ROWS], preferred_element_type=F32)
+    raw += jnp.dot(dbuf[me, :, HALF:], kbuf[1, :, :2 * ROWS], preferred_element_type=F32)
     part[...] = join(raw)
 
     partner = me + 1 - 2 * (me % 2)
@@ -203,18 +204,21 @@
             def _():
                 reduce_copy(k).start()
 
-    fill_field(0, 0, 0)
-
-    @pl.loop(0, KEPT)
-    def _(m):
-        @pl.when(m == FIRST)
-        def _():
-            begin()
-
+    def keep_field(m):
         fill_field(m, 1, 1)
         evaluate_point(0, fst.at[m])
         fill_field((m + 1) % (N - 1), 0, 0)
         evaluate_point(1, fst.at[m])
+
+    fill_field(0, 0, 0)
+
+    @pl.loop(0, EARLY)
+    def _(m):
+        @pl.when(m == FIRST)
+        def _():
+            begin()
+
+        keep_field(m)
 
     def full_copy(k):
         at = spot(me // 2)
@@ -287,11 +291,11 @@
 
     def contract_layer(j, h):
         acc[...] += jnp.dot(
-            dbuf[j, :, h * HALF:(h + 1) * HALF], kbuf[h], preferred_element_type=F32
+            dbuf[j, :, h * HALF:(h + 1) * HALF], kbuf[h, :, :2 * ROWS], preferred_element_type=F32
         )
 
     acc[...] = jnp.zeros_like(acc)
-    kbuf[1] = jnp.zeros((HALF, 2 * ROWS), BF)
+    kbuf[1] = jnp.zeros((HALF, 2 * ROWS + 128), BF)
     prepare(me, 0)
     prepare(me, 1)
     fill_layer(0)
@@ -302,7 +306,7 @@
         before = (1 - some) * me + some * ((partner + 2 * pair + N - 2) % N)
         here = ((me + 2 * pair) % N, (partner + 2 * pair) % N, (me + 2 * pair + 2) % N)
 
-        @pl.when(pair == 0)
+        @pl.when(pair == 1)
         def _():
             finish_amplitudes()
 
@@ -340,6 +344,12 @@
 
     contract_layer((partner + N - 2) % N, 1)
     image = join(acc[...])
+    fill_field(EARLY, 0, 0)
+
+    @pl.loop(EARLY, KEPT)
+    def _(m):
+        keep_field(m)
+
 
     @pl.loop(0, OWNERS)
     def _(o):
@@ -359,8 +369,8 @@
     @pl.loop(0, KEPT)
     def _(m):
         other = (group + 1 + m) % N
-        raw = jnp.dot(far(other, 0), fst[m, 0], preferred_element_type=F32)
-        raw += jnp.dot(far(other, 1), fst[m, 1], preferred_element_type=F32)
+        raw = jnp.dot(far(other, 0), fst[m, 0, :, :2 * ROWS], preferred_element_type=F32)
+        raw += jnp.dot(far(other, 1), fst[m, 1, :, :2 * ROWS], preferred_element_type=F32)
         acc[...] += raw
 
     rhs = live * (inc[...] - KAPPA * join(acc[...]))
@@ -369,15 +379,16 @@
 
     update = (d1buf, s_s, s_r)
 
+    to_partner(*update).start()
+
     @pl.loop(1, chips)
     def _(d):
         to_chip(*update, d).start()
 
-    to_partner(*update).start()
-    acc[...] = jnp.dot(d1buf[me], kst[me], preferred_element_type=F32)
+    acc[...] = jnp.dot(d1buf[me], kst[me, :, :2 * ROWS], preferred_element_type=F32)
 
     def apply(j):
-        acc[...] += jnp.dot(d1buf[j], kst[j], preferred_element_type=F32)
+        acc[...] += jnp.dot(d1buf[j], kst[j, :, :2 * ROWS], preferred_element_type=F32)
 
     to_partner(*update).wait_recv()
     apply(partner)
@@ -443,13 +454,13 @@
         scratch_shapes=[
             V((8, rows), F32),
             V((8, N * rows), F32),
-            V((KEPT, 2, HALF, wide), BF),
+            V((KEPT, 2, HALF, wide + 128), BF),
             V((64, rows), BF),
-            V((2, HALF, rows), F32),
-            V((2, HALF, rows), F32),
-            V((2, HALF, wide), BF),
+            V((2, HALF, rows + 128), F32),
+            V((2, HALF, rows + 128), F32),
+            V((2, HALF, wide + 128), BF),
             V((channels, wide), F32),
-            V((N, rows, wide), BF),
+            V((N, rows, wide + 128), BF),
             V((N, 8, rows), F32),
             V((N, channels, rows), BF),
             V((N, channels, rows), BF),

time: 66.2 us -> 63.9 us (0.965); the launches traced: 65 us -> 63.6 us
  Pallas kernels: 62.2 us -> 60.8 us
    pallas_call x1, Pallas kernels: 62.2 us -> 60.8 us  [per_device(): pl.pallas_call(sweep_kernel, out_shape=(jax.ShapeDtypeStruct((channels, r...]
where the time goes in v4:
time: 63.9 us; the launch traced here: 63.6 us
  Pallas kernels  60.8 us (95%)
  local copies, waits for them, and re-layouts  2.14 us (3%)
  between operations  0.65 us (1%)
    pallas_call x1, Pallas kernels, per_device(): pl.pallas_call(sweep_kernel, out_shape=(jax.ShapeDtypeStruct((channels, r...  60.8 us
    unnamed x4, local copies, waits for them, and re-layouts  2.14 us

profile of v4, /device:TPU:8, one launch (start us, length us, event | category | flops | bytes accessed | tf_op | source)
XLA Modules:
  0.0 63.6 jit_solution(6894136390329048756)
XLA Ops:
  0.6 60.8 %shard_map.86 = (f32[32,512]{1,0:T(8,128)}, f32[32,512]{1,0:T(8,128)}) custom-call(s32[16]{0:T(128)} %counts.1, f32[3,512]{1,0:T(4,128)} %points.1, f32[3,512]{1,0:T(4,128)} %normals.1, f32[1,512]{1,0:T(1,128)} %bitcast.1, f32[3,8192]{1,0:T(4,128)} %sources.1, f32[32,512]{1,0:T(8,128)} %dens.1, f32[32,512]{1,0:T(8,128)} %inc.1), custom_call_target="tpu_custom_call" | custom-call | tf_op jit(solution)/shard_map/pallas_call | solution.py:445
  61.4 0.0 copy-start
  61.4 1.5 %copy.11 = f32[32,512]{1,0:T(8,128)} copy(f32[32,512]{1,0:T(8,128)} %get-tuple-element.4) | data formatting | bytes 131072
  62.9 0.0 copy-done
  62.9 0.6 copy.12
Async XLA Ops:
  61.4 1.5 %copy-start = (f32[32,512]{1,0:T(8,128)S(1)}, f32[32,512]{1,0:T(8,128)}, u32[]{:S(2)}) copy-start(f32[32,512]{1,0:T(8,128)} %get-tuple-element.5) | copy-start | bytes 196612
